TPU v7x, 256 devices: a whole 4x4x8 slice. The times are simulated.
256 devices in a mesh: freq: 8 (over y, x_hi), rec: 32 (over x_lo, z, core).
Axes of the slice: x: 4 (x_hi: 2, x_lo: 2; x = x_hi * 2 + x_lo), y: 4, z: 8, core: 2. Of those that a mesh axis runs over, the one named last changes fastest.
Arguments:
- response: bfloat16 [128, 2, 1792, 1792], P('freq', None, 'rec'), may hold values from -1 to 1, as said below
- direct: float32 [1792, 32, 256], P('rec', 'freq'), may hold values from -6 to 6
- onset: int32 [1792, 32], P('rec', 'freq'), may hold values from 16 to 128
Outputs:
- upgoing: float32 [1792, 32, 256], P('rec', 'freq')
- coda: float32 [1792, 32, 256], P('rec', 'freq')
Inputs may be any that keep to these rules, and one draw needn't show every extreme that they name: response[k, c, r, s] = response[k, c, s, r] for every frequency and part (source-receiver reciprocity).
All inputs are finite; a program needn't handle non-finite values.
Results may differ from a plain program's by a relative error of at most 0.023.
Values may be sent and summed in bfloat16 or wider, within the bound.
A program may use at most 128 MiB of HBM per device.

v0:
```python
import math
import jax
import jax.numpy as jnp
from jax import lax
from jax.sharding import PartitionSpec as P

NF = 128
NT = 256
ITERS = 2


def spectral_tables(length, count):
    samples = jnp.arange(length, dtype=jnp.int32)
    frequency_bins = jnp.arange(1, count + 1, dtype=jnp.int32)
    phase = (samples[:, None] * frequency_bins[None, :] % length).astype(jnp.float32) * (
        2.0 * math.pi / length
    )
    cosine = jnp.cos(phase)
    sine = jnp.sin(phase)
    forward = jnp.stack([cosine, -sine], axis=1)
    inverse = jnp.stack([cosine.T, -sine.T], axis=0) * (2.0 / length)
    return (forward, inverse)


def make_window(onset, length):
    samples = jnp.arange(length, dtype=jnp.int32)
    folded = jnp.minimum(samples, length - samples)
    return (folded[None, None, :] < onset[:, :, None]).astype(jnp.float32)


def to_spectrum(field, forward):
    packed = jnp.einsum("svt,tck->kcvs", field, forward)
    return packed.astype(jnp.bfloat16)


def to_time(spectra, inverse):
    return jnp.einsum("kcvs,ckt->svt", spectra.astype(jnp.float32), inverse)


def complex_apply(block, spectra, conj_sign):
    parts = jnp.einsum("fcrs,fdvs->cdfvr", block, spectra, preferred_element_type=jnp.float32)
    real_out = parts[0, 0] - conj_sign * parts[1, 1]
    imag_out = parts[0, 1] + conj_sign * parts[1, 0]
    return jnp.stack([real_out, imag_out], axis=1)


def body(response, direct, onset):
    forward, inverse = spectral_tables(NT, NF)
    window = make_window(onset, NT)
    coda = jnp.zeros_like(direct)
    upgoing = coda
    for iteration in range(ITERS):
        downgoing = direct + coda
        sources = lax.all_to_all(
            to_spectrum(downgoing, forward), "freq", split_axis=0, concat_axis=2, tiled=True
        )
        gathered = lax.all_gather(sources, "rec", axis=3, tiled=True)
        reflected = complex_apply(response, gathered, 1.0)
        reflected_time = lax.all_to_all(
            reflected.astype(jnp.bfloat16), "freq", split_axis=2, concat_axis=0, tiled=True
        )
        upgoing = window * to_time(reflected_time, inverse)
        spectra_up = lax.all_to_all(
            to_spectrum(upgoing, forward), "freq", split_axis=0, concat_axis=2, tiled=True
        )
        receivers = lax.all_gather(spectra_up, "rec", axis=3, tiled=True)
        returned = complex_apply(response, receivers, -1.0)
        returned_time = lax.all_to_all(
            returned.astype(jnp.bfloat16), "freq", split_axis=2, concat_axis=0, tiled=True
        )
        coda = window * to_time(returned_time, inverse)
    return (upgoing, coda)


def solution(mesh):
    placed = (P("freq", None, "rec", None), P("rec", "freq", None), P("rec", "freq"))
    return jax.shard_map(
        body,
        mesh=mesh,
        in_specs=placed,
        out_specs=(P("rec", "freq", None), P("rec", "freq", None)),
        check_vma=False,
    )
```

profile of v0, /device:TPU:96, one launch (start us, length us, event | category | flops | bytes accessed | tf_op | source)
XLA Modules:
  0.0 545.7 jit_solution(14085154062390279766)
XLA Ops:
  7.8 1.1 fusion.39
  9.5 14.9 %all_to_all.144 = bf16[8,2,3584]{2,1,0:T(2,128)(2,1)S(1)} all-to-all(bf16[8,2,3584]{2,1,0:T(2,128)(2,1)S(1)} %reshape.396), channel_id=1, replica_groups=mesh['freq'=8,'rec'=32] {'freq'}, dimensions={0} | all-to-all | bytes 229376 | tf_op jit(solution)/shard_map/all_to_all | solution.py:54
  24.9 1.5 copy.89
  27.0 87.4 %all-gather.5.cloned.1.call-done = bf16[16,2,32,1792]{2,0,1,3:T(8,128)(2,1)} async-done(((bf16[16,2,32,56]{2,0,1,3:T(8,128)(2,1)}), bf16[16,2,32,1792]{2,0,1,3:T(8,128)(2,1)}) %all-gather.5.cloned.1.call-update) | async-done | bytes 3670032 | tf_op jit(solution)/shard_map/all_gather | solution.py:57
  114.4 15.0 %fusion.17 = f32[2,2,16,32,56]{4,3,0,1,2:T(8,128)S(1)} fusion(bf16[16,2,56,1792]{3,2,1,0:T(8,128)(2,1)} %param.3, bf16[16,2,32,1792,1]{2,0,1,3,4:T(8,128)(2,1)} %bitcast.271), kind=kOutput, calls=%fused_computation.13 | convolution fusion | flops 411041792 | bytes 10551296 | tf_op jit(solution)/shard_map/fcrs,fdvs->cdfvr/dot_general | solution.py:41
  129.7 1.1 reshape.398
  130.8 6.7 %all-to-all-start.1 = ((bf16[8,2,3584]{2,1,0:T(2,128)(2,1)}), bf16[8,2,3584]{2,1,0:T(2,128)(2,1)S(1)}, u32[]{:S(2)}, u32[]{:S(2)}) async-start(bf16[8,2,3584]{2,1,0:T(2,128)(2,1)} %reshape.398), calls=%async_computation.1 | async-start | bytes 229376 | tf_op jit(solution)/shard_map/all_to_all | solution.py:59
  137.6 8.1 %all-to-all-done.1 = bf16[8,2,3584]{2,1,0:T(2,128)(2,1)S(1)} async-done(((bf16[8,2,3584]{2,1,0:T(2,128)(2,1)}), bf16[8,2,3584]{2,1,0:T(2,128)(2,1)S(1)}, u32[]{:S(2)}, u32[]{:S(2)}) %all-to-all-start.1) | async-done | bytes 114720 | tf_op jit(solution)/shard_map/all_to_all | solution.py:59
  147.1 10.5 %all_to_all.145 = bf16[8,2,3584]{2,1,0:T(2,128)(2,1)S(1)} all-to-all(bf16[8,2,3584]{2,1,0:T(2,128)(2,1)S(1)} %reshape.400), channel_id=1, replica_groups=mesh['freq'=8,'rec'=32] {'freq'}, dimensions={0} | all-to-all | bytes 229376 | tf_op jit(solution)/shard_map/all_to_all | solution.py:63
  158.2 1.5 copy.99
  159.9 85.8 %all-gather.7.cloned.1.call-done = bf16[16,2,32,1792]{2,0,1,3:T(8,128)(2,1)} async-done(((bf16[16,2,32,56]{2,0,1,3:T(8,128)(2,1)}), bf16[16,2,32,1792]{2,0,1,3:T(8,128)(2,1)}) %all-gather.7.cloned.1.call-update) | async-done | bytes 3670032 | tf_op jit(solution)/shard_map/all_gather | solution.py:66
  245.6 15.1 %fusion.22 = f32[2,2,16,32,56]{4,3,0,1,2:T(8,128)S(1)} fusion(bf16[16,2,56,1792]{3,2,1,0:T(8,128)(2,1)} %param.3, bf16[16,2,32,1792,1]{2,0,1,3,4:T(8,128)(2,1)} %bitcast.272), kind=kOutput, calls=%fused_computation.14 | convolution fusion | flops 411041792 | bytes 10551296 | tf_op jit(solution)/shard_map/fcrs,fdvs->cdfvr/dot_general | solution.py:41
  261.4 14.6 %all_to_all.146 = bf16[8,2,3584]{2,1,0:T(2,128)(2,1)S(1)} all-to-all(bf16[8,2,3584]{2,1,0:T(2,128)(2,1)S(1)} %reshape.402), channel_id=1, replica_groups=mesh['freq'=8,'rec'=32] {'freq'}, dimensions={0} | all-to-all | bytes 229376 | tf_op jit(solution)/shard_map/all_to_all | solution.py:68
  277.5 10.5 %all_to_all.147 = bf16[8,2,3584]{2,1,0:T(2,128)(2,1)S(1)} all-to-all(bf16[8,2,3584]{2,1,0:T(2,128)(2,1)S(1)} %reshape.404), channel_id=1, replica_groups=mesh['freq'=8,'rec'=32] {'freq'}, dimensions={0} | all-to-all | bytes 229376 | tf_op jit(solution)/shard_map/all_to_all | solution.py:54
  288.6 1.5 copy.111
  290.3 85.7 %all-gather.9.cloned.1.call-done = bf16[16,2,32,1792]{2,0,1,3:T(8,128)(2,1)} async-done(((bf16[16,2,32,56]{2,0,1,3:T(8,128)(2,1)}), bf16[16,2,32,1792]{2,0,1,3:T(8,128)(2,1)}) %all-gather.9.cloned.1.call-update) | async-done | bytes 3670032 | tf_op jit(solution)/shard_map/all_gather | solution.py:57
  376.0 15.0 %fusion.27 = f32[2,2,16,32,56]{4,3,0,1,2:T(8,128)S(1)} fusion(bf16[16,2,56,1792]{3,2,1,0:T(8,128)(2,1)} %param.3, bf16[16,2,32,1792,1]{2,0,1,3,4:T(8,128)(2,1)} %bitcast.273), kind=kOutput, calls=%fused_computation.15 | convolution fusion | flops 411041792 | bytes 10551296 | tf_op jit(solution)/shard_map/fcrs,fdvs->cdfvr/dot_general | solution.py:41
  391.8 14.6 %all_to_all.148 = bf16[8,2,3584]{2,1,0:T(2,128)(2,1)S(1)} all-to-all(bf16[8,2,3584]{2,1,0:T(2,128)(2,1)S(1)} %reshape.406), channel_id=1, replica_groups=mesh['freq'=8,'rec'=32] {'freq'}, dimensions={0} | all-to-all | bytes 229376 | tf_op jit(solution)/shard_map/all_to_all | solution.py:59
  407.9 10.5 %all_to_all.149 = bf16[8,2,3584]{2,1,0:T(2,128)(2,1)S(1)} all-to-all(bf16[8,2,3584]{2,1,0:T(2,128)(2,1)S(1)} %reshape.408), channel_id=1, replica_groups=mesh['freq'=8,'rec'=32] {'freq'}, dimensions={0} | all-to-all | bytes 229376 | tf_op jit(solution)/shard_map/all_to_all | solution.py:63
  419.0 1.5 copy.121
  420.5 86.0 %all-gather.11.cloned.1.call-done = bf16[16,2,32,1792]{2,0,1,3:T(8,128)(2,1)} async-done(((bf16[16,2,32,56]{2,0,1,3:T(8,128)(2,1)}), bf16[16,2,32,1792]{2,0,1,3:T(8,128)(2,1)}) %all-gather.11.cloned.1.call-update) | async-done | bytes 3670032 | tf_op jit(solution)/shard_map/all_gather | solution.py:66
  506.5 15.0 %fusion.12 = f32[2,2,16,32,56]{4,3,2,1,0:T(8,128)S(1)} fusion(bf16[16,2,32,1792,1]{2,0,1,3,4:T(8,128)(2,1)} %bitcast.274, bf16[16,2,56,1792]{3,2,1,0:T(8,128)(2,1)} %param.3), kind=kOutput, calls=%fused_computation.12 | convolution fusion | flops 411041792 | bytes 10551296 | tf_op jit(solution)/shard_map/fcrs,fdvs->cdfvr/dot_general | solution.py:41
  522.8 6.7 %all-to-all-start.7 = ((bf16[8,2,3584]{2,1,0:T(2,128)(2,1)}), bf16[8,2,3584]{2,1,0:T(2,128)(2,1)S(1)}, u32[]{:S(2)}, u32[]{:S(2)}) async-start(bf16[8,2,3584]{2,1,0:T(2,128)(2,1)} %reshape.410), calls=%async_computation.7 | async-start | bytes 229376 | tf_op jit(solution)/shard_map/all_to_all | solution.py:68
  530.3 7.4 %all-to-all-done.7 = bf16[8,2,3584]{2,1,0:T(2,128)(2,1)S(1)} async-done(((bf16[8,2,3584]{2,1,0:T(2,128)(2,1)}), bf16[8,2,3584]{2,1,0:T(2,128)(2,1)S(1)}, u32[]{:S(2)}, u32[]{:S(2)}) %all-to-all-start.7) | async-done | bytes 114720 | tf_op jit(solution)/shard_map/all_to_all | solution.py:68
  (69 shorter events, 13.9 us)
Async XLA Ops:
  7.2 107.3 %all-gather.5.cloned.1.call-start = ((), (), s32[]{:S(2)}) async-start(), calls=%async_computation.8 | async-start | bytes 15138816 | tf_op jit(solution)/shard_map/all_gather | solution.py:57
  114.4 31.7 %copy-start.1 = (s32[56,4]{0,1:T(4,128)S(1)}, s32[56,4]{0,1:T(4,128)}, u32[]{:S(2)}) copy-start(s32[56,4]{0,1:T(4,128)} %param.5) | copy-start | bytes 2692
  130.8 14.8 %all-to-all-start.1 = ((bf16[8,2,3584]{2,1,0:T(2,128)(2,1)}), bf16[8,2,3584]{2,1,0:T(2,128)(2,1)S(1)}, u32[]{:S(2)}, u32[]{:S(2)}) async-start(bf16[8,2,3584]{2,1,0:T(2,128)(2,1)} %reshape.398), calls=%async_computation.1 | async-start | bytes 229376 | tf_op jit(solution)/shard_map/all_to_all | solution.py:59
  137.5 108.1 %all-gather.7.cloned.1.call-start = ((), (), s32[]{:S(2)}) async-start(), calls=%async_computation.9 | async-start | bytes 15138816 | tf_op jit(solution)/shard_map/all_gather | solution.py:66
  159.6 216.4 %all-gather.9.cloned.1.call-start = ((), (), s32[]{:S(2)}) async-start(), calls=%async_computation.10 | async-start | bytes 15138816 | tf_op jit(solution)/shard_map/all_gather | solution.py:57
  245.6 30.9 %copy-start = (f32[56,4,256]{2,1,0:T(4,128)S(1)}, f32[56,4,256]{2,1,0:T(4,128)}, u32[]{:S(2)}) copy-start(f32[56,4,256]{2,1,0:T(4,128)} %param.4) | copy-start | bytes 688132
  290.1 216.4 %all-gather.11.cloned.1.call-start = ((), (), s32[]{:S(2)}) async-start(), calls=%async_computation.11 | async-start | bytes 15138816 | tf_op jit(solution)/shard_map/all_gather | solution.py:66
  522.8 14.8 %all-to-all-start.7 = ((bf16[8,2,3584]{2,1,0:T(2,128)(2,1)}), bf16[8,2,3584]{2,1,0:T(2,128)(2,1)S(1)}, u32[]{:S(2)}, u32[]{:S(2)}) async-start(bf16[8,2,3584]{2,1,0:T(2,128)(2,1)} %reshape.410), calls=%async_computation.7 | async-start | bytes 229376 | tf_op jit(solution)/shard_map/all_to_all | solution.py:68
Sparse Core Ops, SparseCore 0:
  26.5 87.8 all-gather.4
  159.8 85.8 all-gather.6
  290.2 85.8 all-gather.8
  420.6 85.8 all-gather.10
where the time goes:
time: 546 us
  waiting for transfers between devices  360 us (66%)
  blocking collectives  75.7 us (14%)
  matrix products  62.6 us (11%)
  local copies, waits for them, and re-layouts  17 us (3%)
  between operations  14.2 us (3%)
  starting transfers between devices  14 us (3%)
    all_gather x2, waiting for transfers between devices, body(): gathered = lax.all_gather(sources, 'rec', axis=3, tiled=True)  173 us
    all_gather x2, waiting for transfers between devices, body(): receivers = lax.all_gather(spectra_up, 'rec', axis=3, tiled=True)  172 us
    dot_general x4, matrix products, complex_apply(): jnp.einsum('fcrs,fdvs->cdfvr', block, spectra, preferred_element_type=jnp...  60.1 us
    all_to_all x2, blocking collectives, body(): lax.all_to_all(to_spectrum(downgoing, forward), 'freq', split_axis=0, con...  25.4 us
    all_to_all x2, blocking collectives, body(): lax.all_to_all(to_spectrum(upgoing, forward), 'freq', split_axis=0, conca...  21.1 us
    all_to_all x1, blocking collectives, body(): lax.all_to_all(reflected.astype(jnp.bfloat16), 'freq', split_axis=2, conc...  14.6 us
    all_to_all x1, blocking collectives, body(): lax.all_to_all(returned.astype(jnp.bfloat16), 'freq', split_axis=2, conca...  14.6 us
  transfers between devices with their start and end apart: 6, of which 6 were waited for; matrix products, arithmetic and copies ran while one was open for 0% of the time, Pallas kernels for 0%

commit v1 on v0

--- a/solution.py
+++ b/solution.py
@@ -65,8 +65,14 @@
         )
         receivers = lax.all_gather(spectra_up, "rec", axis=3, tiled=True)
         returned = complex_apply(response, receivers, -1.0)
-        returned_time = lax.all_to_all(
-            returned.astype(jnp.bfloat16), "freq", split_axis=2, concat_axis=0, tiled=True
+        returned_time = jnp.concatenate(
+            lax.all_to_all(
+                jnp.stack(jnp.split(returned.astype(jnp.bfloat16), lax.axis_size("freq"), axis=2)),
+                "freq",
+                0,
+                0,
+            ),
+            axis=0,
         )
         coda = window * to_time(returned_time, inverse)
     return (upgoing, coda)

time: 546 us -> 547 us (level)
  no operation moved by 1% of the time
where the time goes in v1:
time: 547 us; the launch traced here: 546 us
  waiting for transfers between devices  360 us (66%)
  blocking collectives  75.7 us (14%)
  matrix products  62.7 us (11%)
  local copies, waits for them, and re-layouts  16.8 us (3%)
  between operations  14.2 us (3%)
  starting transfers between devices  14 us (3%)
    all_gather x2, waiting for transfers between devices, body(): gathered = lax.all_gather(sources, 'rec', axis=3, tiled=True)  173 us
    all_gather x2, waiting for transfers between devices, body(): receivers = lax.all_gather(spectra_up, 'rec', axis=3, tiled=True)  172 us
    dot_general x4, matrix products, complex_apply(): jnp.einsum('fcrs,fdvs->cdfvr', block, spectra, preferred_element_type=jnp...  60.1 us
    all_to_all x2, blocking collectives, body(): lax.all_to_all(to_spectrum(downgoing, forward), 'freq', split_axis=0, con...  25.4 us
    all_to_all x2, blocking collectives, body(): lax.all_to_all(to_spectrum(upgoing, forward), 'freq', split_axis=0, conca...  21.1 us
    all_to_all x1, blocking collectives, body(): lax.all_to_all(reflected.astype(jnp.bfloat16), 'freq', split_axis=2, conc...  14.6 us
    all_to_all x1, blocking collectives, body(): lax.all_to_all(jnp.stack(jnp.split(returned.astype(jnp.bfloat16), lax.axi...  14.6 us
  transfers between devices with their start and end apart: 6, of which 6 were waited for; matrix products, arithmetic and copies ran while one was open for 0% of the time, Pallas kernels for 0%

profile of v1, /device:TPU:96, one launch (start us, length us, event | category | flops | bytes accessed | tf_op | source)
XLA Modules:
  0.0 546.0 jit_solution(10637572400658094554)
XLA Ops:
  7.8 1.1 fusion.39
  9.5 14.9 %all_to_all.118 = bf16[8,2,3584]{2,1,0:T(2,128)(2,1)S(1)} all-to-all(bf16[8,2,3584]{2,1,0:T(2,128)(2,1)S(1)} %reshape.404), channel_id=1, replica_groups=mesh['freq'=8,'rec'=32] {'freq'}, dimensions={0} | all-to-all | bytes 229376 | tf_op jit(solution)/shard_map/all_to_all | solution.py:54
  24.9 1.5 copy.86
  27.0 87.4 %all-gather.5.cloned.1.call-done = bf16[16,2,32,1792]{2,0,1,3:T(8,128)(2,1)} async-done(((bf16[16,2,32,56]{2,0,1,3:T(8,128)(2,1)}), bf16[16,2,32,1792]{2,0,1,3:T(8,128)(2,1)}) %all-gather.5.cloned.1.call-update) | async-done | bytes 3670032 | tf_op jit(solution)/shard_map/all_gather | solution.py:57
  114.4 15.0 %fusion.17 = f32[2,2,16,32,56]{4,3,0,1,2:T(8,128)S(1)} fusion(bf16[16,2,56,1792]{3,2,1,0:T(8,128)(2,1)} %param.3, bf16[16,2,32,1792,1]{2,0,1,3,4:T(8,128)(2,1)} %bitcast.293), kind=kOutput, calls=%fused_computation.13 | convolution fusion | flops 411041792 | bytes 10551296 | tf_op jit(solution)/shard_map/fcrs,fdvs->cdfvr/dot_general | solution.py:41
  130.8 6.7 %all-to-all-start.1 = ((bf16[8,2,3584]{2,1,0:T(2,128)(2,1)}), bf16[8,2,3584]{2,1,0:T(2,128)(2,1)S(1)}, u32[]{:S(2)}, u32[]{:S(2)}) async-start(bf16[8,2,3584]{2,1,0:T(2,128)(2,1)} %reshape.406), calls=%async_computation.1 | async-start | bytes 229376 | tf_op jit(solution)/shard_map/all_to_all | solution.py:59
  137.6 8.1 %all-to-all-done.1 = bf16[8,2,3584]{2,1,0:T(2,128)(2,1)S(1)} async-done(((bf16[8,2,3584]{2,1,0:T(2,128)(2,1)}), bf16[8,2,3584]{2,1,0:T(2,128)(2,1)S(1)}, u32[]{:S(2)}, u32[]{:S(2)}) %all-to-all-start.1) | async-done | bytes 114720 | tf_op jit(solution)/shard_map/all_to_all | solution.py:59
  147.1 10.5 %all_to_all.119 = bf16[8,2,3584]{2,1,0:T(2,128)(2,1)S(1)} all-to-all(bf16[8,2,3584]{2,1,0:T(2,128)(2,1)S(1)} %reshape.408), channel_id=1, replica_groups=mesh['freq'=8,'rec'=32] {'freq'}, dimensions={0} | all-to-all | bytes 229376 | tf_op jit(solution)/shard_map/all_to_all | solution.py:63
  158.2 1.5 copy.96
  159.9 85.8 %all-gather.7.cloned.1.call-done = bf16[16,2,32,1792]{2,0,1,3:T(8,128)(2,1)} async-done(((bf16[16,2,32,56]{2,0,1,3:T(8,128)(2,1)}), bf16[16,2,32,1792]{2,0,1,3:T(8,128)(2,1)}) %all-gather.7.cloned.1.call-update) | async-done | bytes 3670032 | tf_op jit(solution)/shard_map/all_gather | solution.py:66
  245.7 15.1 %fusion.22 = f32[2,2,16,32,56]{4,3,0,1,2:T(8,128)S(1)} fusion(bf16[16,2,56,1792]{3,2,1,0:T(8,128)(2,1)} %param.3, bf16[16,2,32,1792,1]{2,0,1,3,4:T(8,128)(2,1)} %bitcast.294), kind=kOutput, calls=%fused_computation.14 | convolution fusion | flops 411041792 | bytes 10551296 | tf_op jit(solution)/shard_map/fcrs,fdvs->cdfvr/dot_general | solution.py:41
  261.5 14.6 %all_to_all.120 = bf16[8,2,3584]{2,1,0:T(2,128)(2,1)S(1)} all-to-all(bf16[8,2,3584]{2,1,0:T(2,128)(2,1)S(1)} %reshape.410), channel_id=1, replica_groups=mesh['freq'=8,'rec'=32] {'freq'}, dimensions={0} | all-to-all | bytes 229376 | tf_op jit(solution)/shard_map/all_to_all | solution.py:69
  277.6 10.5 %all_to_all.121 = bf16[8,2,3584]{2,1,0:T(2,128)(2,1)S(1)} all-to-all(bf16[8,2,3584]{2,1,0:T(2,128)(2,1)S(1)} %reshape.412), channel_id=1, replica_groups=mesh['freq'=8,'rec'=32] {'freq'}, dimensions={0} | all-to-all | bytes 229376 | tf_op jit(solution)/shard_map/all_to_all | solution.py:54
  288.7 1.5 copy.107
  290.4 85.7 %all-gather.9.cloned.1.call-done = bf16[16,2,32,1792]{2,0,1,3:T(8,128)(2,1)} async-done(((bf16[16,2,32,56]{2,0,1,3:T(8,128)(2,1)}), bf16[16,2,32,1792]{2,0,1,3:T(8,128)(2,1)}) %all-gather.9.cloned.1.call-update) | async-done | bytes 3670032 | tf_op jit(solution)/shard_map/all_gather | solution.py:57
  376.2 15.0 %fusion.27 = f32[2,2,16,32,56]{4,3,0,1,2:T(8,128)S(1)} fusion(bf16[16,2,56,1792]{3,2,1,0:T(8,128)(2,1)} %param.3, bf16[16,2,32,1792,1]{2,0,1,3,4:T(8,128)(2,1)} %bitcast.295), kind=kOutput, calls=%fused_computation.15 | convolution fusion | flops 411041792 | bytes 10551296 | tf_op jit(solution)/shard_map/fcrs,fdvs->cdfvr/dot_general | solution.py:41
  391.9 14.6 %all_to_all.122 = bf16[8,2,3584]{2,1,0:T(2,128)(2,1)S(1)} all-to-all(bf16[8,2,3584]{2,1,0:T(2,128)(2,1)S(1)} %reshape.414), channel_id=1, replica_groups=mesh['freq'=8,'rec'=32] {'freq'}, dimensions={0} | all-to-all | bytes 229376 | tf_op jit(solution)/shard_map/all_to_all | solution.py:59
  408.1 10.5 %all_to_all.123 = bf16[8,2,3584]{2,1,0:T(2,128)(2,1)S(1)} all-to-all(bf16[8,2,3584]{2,1,0:T(2,128)(2,1)S(1)} %reshape.416), channel_id=1, replica_groups=mesh['freq'=8,'rec'=32] {'freq'}, dimensions={0} | all-to-all | bytes 229376 | tf_op jit(solution)/shard_map/all_to_all | solution.py:63
  419.1 1.5 copy.117
  420.6 86.0 %all-gather.11.cloned.1.call-done = bf16[16,2,32,1792]{2,0,1,3:T(8,128)(2,1)} async-done(((bf16[16,2,32,56]{2,0,1,3:T(8,128)(2,1)}), bf16[16,2,32,1792]{2,0,1,3:T(8,128)(2,1)}) %all-gather.11.cloned.1.call-update) | async-done | bytes 3670032 | tf_op jit(solution)/shard_map/all_gather | solution.py:66
  506.6 15.0 %fusion.12 = f32[2,2,16,32,56]{4,3,2,1,0:T(8,128)S(1)} fusion(bf16[16,2,32,1792,1]{2,0,1,3,4:T(8,128)(2,1)} %bitcast.296, bf16[16,2,56,1792]{3,2,1,0:T(8,128)(2,1)} %param.3), kind=kOutput, calls=%fused_computation.12 | convolution fusion | flops 411041792 | bytes 10551296 | tf_op jit(solution)/shard_map/fcrs,fdvs->cdfvr/dot_general | solution.py:41
  522.0 1.1 reshape.418
  523.1 6.7 %all-to-all-start.7 = ((bf16[8,2,3584]{2,1,0:T(2,128)(2,1)}), bf16[8,2,3584]{2,1,0:T(2,128)(2,1)S(1)}, u32[]{:S(2)}, u32[]{:S(2)}) async-start(bf16[8,2,3584]{2,1,0:T(2,128)(2,1)} %reshape.418), calls=%async_computation.7 | async-start | bytes 229376 | tf_op jit(solution)/shard_map/all_to_all | solution.py:69
  530.5 7.4 %all-to-all-done.7 = bf16[8,2,3584]{2,1,0:T(2,128)(2,1)S(1)} async-done(((bf16[8,2,3584]{2,1,0:T(2,128)(2,1)}), bf16[8,2,3584]{2,1,0:T(2,128)(2,1)S(1)}, u32[]{:S(2)}, u32[]{:S(2)}) %all-to-all-start.7) | async-done | bytes 114720 | tf_op jit(solution)/shard_map/all_to_all | solution.py:69
  (81 shorter events, 14.1 us)
Async XLA Ops:
  7.2 107.3 %all-gather.5.cloned.1.call-start = ((), (), s32[]{:S(2)}) async-start(), calls=%async_computation.8 | async-start | bytes 15138816 | tf_op jit(solution)/shard_map/all_gather | solution.py:57
  114.4 31.7 %copy-start = (s32[56,4]{0,1:T(4,128)S(1)}, s32[56,4]{0,1:T(4,128)}, u32[]{:S(2)}) copy-start(s32[56,4]{0,1:T(4,128)} %param.5) | copy-start | bytes 2692
  130.8 14.8 %all-to-all-start.1 = ((bf16[8,2,3584]{2,1,0:T(2,128)(2,1)}), bf16[8,2,3584]{2,1,0:T(2,128)(2,1)S(1)}, u32[]{:S(2)}, u32[]{:S(2)}) async-start(bf16[8,2,3584]{2,1,0:T(2,128)(2,1)} %reshape.406), calls=%async_computation.1 | async-start | bytes 229376 | tf_op jit(solution)/shard_map/all_to_all | solution.py:59
  137.5 108.1 %all-gather.7.cloned.1.call-start = ((), (), s32[]{:S(2)}) async-start(), calls=%async_computation.9 | async-start | bytes 15138816 | tf_op jit(solution)/shard_map/all_gather | solution.py:66
  159.7 216.5 %all-gather.9.cloned.1.call-start = ((), (), s32[]{:S(2)}) async-start(), calls=%async_computation.10 | async-start | bytes 15138816 | tf_op jit(solution)/shard_map/all_gather | solution.py:57
  245.7 31.0 %copy-start.1 = (f32[56,4,256]{2,1,0:T(4,128)S(1)}, f32[56,4,256]{2,1,0:T(4,128)}, u32[]{:S(2)}) copy-start(f32[56,4,256]{2,1,0:T(4,128)} %param.4) | copy-start | bytes 688132
  290.2 216.4 %all-gather.11.cloned.1.call-start = ((), (), s32[]{:S(2)}) async-start(), calls=%async_computation.11 | async-start | bytes 15138816 | tf_op jit(solution)/shard_map/all_gather | solution.py:66
  523.1 14.8 %all-to-all-start.7 = ((bf16[8,2,3584]{2,1,0:T(2,128)(2,1)}), bf16[8,2,3584]{2,1,0:T(2,128)(2,1)S(1)}, u32[]{:S(2)}, u32[]{:S(2)}) async-start(bf16[8,2,3584]{2,1,0:T(2,128)(2,1)} %reshape.418), calls=%async_computation.7 | async-start | bytes 229376 | tf_op jit(solution)/shard_map/all_to_all | solution.py:69
Sparse Core Ops, SparseCore 0:
  26.5 87.8 all-gather.4
  159.8 85.8 all-gather.6
  290.3 85.8 all-gather.8
  420.7 85.8 all-gather.10
